TPU v7x, 512 devices: a whole 4x4x16 slice. The times are simulated.
512 devices in a mesh: prow: 16 (over z), pcol: 32 (over x, y, core).
Axes of the slice: x: 4, y: 4, z: 16, core: 2. Of those that a mesh axis runs over, the one named last changes fastest.
Arguments:
- matrix: float32 [8192, 32768], P('prow', 'pcol'), may hold values from -6 to 6
- pivot_inverse: float32 [2, 512, 512], P(None, 'prow'), may hold values from -0.01171875 to 0.01171875
- row_live: int32 [2, 16], replicated, may hold values 0 or 1
- col_live: int32 [2, 64], replicated, may hold values 0 or 1
Outputs:
- factored: float32 [8192, 32768], P('prow', 'pcol')
All inputs are finite; a program needn't handle non-finite values.
Results may differ from a plain program's by a relative error of at most 0.0001.
Values sent between devices are 32-bit elements; how exact they have to be, the bound alone decides.
No kernel may reach another device: no remote copies, remote signals or barrier semaphores. Data moves between devices by JAX's collectives and lax.ppermute only.
A program may use at most 64 MiB of HBM per device.

v0:
```python
import jax
import jax.numpy as jnp
from jax import lax
from jax.sharding import PartitionSpec as P


def copy_for_each(value, axis):
    copies = jnp.broadcast_to(value, (lax.axis_size(axis), *value.shape))
    return lax.all_to_all(copies, axis, split_axis=0, concat_axis=0, tiled=True)


def laid_out(tiles, dim):
    tiles = jnp.moveaxis(tiles, 0, dim)
    dims = tiles.shape
    return tiles.reshape(*dims[:dim], dims[dim] * dims[dim + 1], *dims[dim + 2 :])


def gathered_copies(value, axis, dim):
    tiles = copy_for_each(value, axis)
    return laid_out(tiles, dim)


def spread(value, axis, source):
    kept = jnp.where(lax.axis_index(axis) == source, value, 0).astype(value.dtype)
    return lax.psum(kept, axis)


def filled_up(lines, length):
    spare = -lines.shape[0] % length
    if not spare:
        return lines
    return jnp.concatenate([lines, jnp.zeros((spare, *lines.shape[1:]), lines.dtype)])


def broadcast_by_parts(value, axis, root):
    lines = jnp.where(lax.axis_index(axis) == root, value, jnp.zeros_like(value)).reshape(
        -1, *value.shape[1:][-1:]
    )
    padded = filled_up(lines, lax.axis_size(axis))
    own = lax.psum_scatter(padded, axis, scatter_dimension=0, tiled=True)
    return lax.all_gather(own, axis, axis=0, tiled=True)[: len(lines)].reshape(value.shape)


def apply_pivot(column_part, pivot_rows):
    return jnp.einsum(
        "rbc,cd->rbd",
        column_part,
        gathered_copies(pivot_rows, "prow", 0),
        precision=lax.Precision.HIGHEST,
    )


def per_device(matrix, pivot_inverse, row_live, col_live):
    block_width = pivot_inverse.shape[2]
    row_blocks = matrix.shape[0] // block_width
    col_blocks = matrix.shape[1] // block_width
    pcol_here = lax.axis_index("pcol")
    row_index = jnp.arange(row_blocks, dtype=jnp.int32) * lax.axis_size("prow") + lax.axis_index(
        "prow"
    )
    col_index = jnp.arange(col_blocks, dtype=jnp.int32) * lax.axis_size("pcol") + pcol_here
    blocks = matrix.reshape(row_blocks, block_width, col_blocks, block_width)

    def lower_panel(column_part, panel):
        row_mask = jnp.where(row_index > panel, jnp.take(row_live[panel], row_index), 0).astype(
            jnp.float32
        )[:, None, None]
        received = spread(column_part, "pcol", panel)
        return apply_pivot(received, pivot_inverse[panel]) * row_mask

    def upper_row(current, panel):
        col_mask = jnp.where(col_index > panel, jnp.take(col_live[panel], col_index), 0).astype(
            jnp.float32
        )
        return broadcast_by_parts(current[0] * col_mask[None, :, None], "prow", panel)

    def store_lower(column_part, lower_part, panel):
        keep_rows = (row_index > panel)[:, None, None] & (pcol_here == panel)
        return jnp.where(keep_rows, lower_part, column_part)

    def outer_update(current, lower_part, upper_part):
        return current - jnp.einsum(
            "rbc,cjd->rbjd", lower_part, upper_part, precision=lax.Precision.HIGHEST
        )

    lower_part = lower_panel(blocks[:, :, 0, :], 0)
    upper_part = upper_row(blocks, 0)
    blocks = outer_update(blocks, lower_part, upper_part)
    blocks = blocks.at[:, :, 0, :].set(store_lower(blocks[:, :, 0, :], lower_part, 0))
    next_lower = lower_panel(blocks[:, :, 0, :], 1)
    next_upper = upper_row(blocks, 1)
    blocks = outer_update(blocks, next_lower, next_upper)
    blocks = blocks.at[:, :, 0, :].set(store_lower(blocks[:, :, 0, :], next_lower, 1))
    return blocks.reshape(row_blocks * block_width, col_blocks * block_width)


def solution(mesh):
    in_specs = (P("prow", "pcol"), P(None, "prow", None), P(), P())
    out_specs = P("prow", "pcol")
    return jax.shard_map(
        per_device, mesh=mesh, in_specs=in_specs, out_specs=out_specs, check_vma=False
    )
```

profile of v0, /device:TPU:4, one launch (start us, length us, event | category | flops | bytes accessed | tf_op | source)
XLA Modules:
  0.0 403.3 jit_solution(14999764444500926546)
XLA Ops:
  7.4 0.8 slice_bitcast_fusion.4
  8.1 0.6 gather_fusion
  8.8 0.6 gather_fusion.1
  9.5 0.2 mul.56
  9.6 1.7 squeeze_reshape.3
  11.4 1.5 multiply_select_fusion.1
  12.9 0.0 reduce-scatter.3.cloned.1.call-update
  12.9 0.0 all-reduce.3.cloned.1.call-start
  13.0 1.5 copy-done
  14.5 2.8 reshape.162
  17.3 2.5 broadcast_select_fusion
  19.8 1.1 copy.28
  20.8 0.0 all-reduce.3.cloned.1.call-update
  20.9 1.1 broadcast_in_dim.55
  22.0 15.2 %all-to-all-start = ((f32[16,32,512]{2,1,0:T(8,128)}), f32[16,32,512]{2,1,0:T(8,128)S(1)}, u32[]{:S(2)}, u32[]{:S(2)}) async-start(f32[16,32,512]{2,1,0:T(8,128)} %broadcast_in_dim.55), calls=%async_computation | async-start | bytes 2097152 | tf_op jit(solution)/shard_map/all_to_all | solution.py:9
  37.2 0.0 all-gather.3.cloned.1.call-start
  37.2 85.9 %reduce-scatter.3.cloned.1.call-done = f32[64,512]{1,0:T(8,128)} async-done(((f32[1024,512]{1,0:T(8,128)}), f32[64,512]{1,0:T(8,128)}) %reduce-scatter.3.cloned.1.call-update) | async-done | bytes 131088 | tf_op jit(solution)/shard_map/reduce_scatter | solution.py:40
  123.2 0.0 all-gather.3.cloned.1.call-update
  123.2 0.2 reduce-scatter.5.cloned.1.call-start
  123.4 1.8 copy.7
  125.3 0.6 fusion.18
  126.5 2.9 copy.9
  129.5 0.2 mul.63
  129.6 32.3 %all-reduce.3.cloned.1.call-done = f32[512,512]{1,0:T(8,128)} async-done(((f32[512,512]{1,0:T(8,128)}), f32[512,512]{1,0:T(8,128)}) %all-reduce.3.cloned.1.call-update) | async-done | bytes 1048592 | tf_op jit(solution)/shard_map/psum | solution.py:25
  162.0 1.0 copy-done.1
  162.9 3.4 convolution_multiply_fusion.1
  166.3 29.4 %all-gather.3.cloned.1.call-done = f32[1024,512]{1,0:T(8,128)} async-done(((f32[64,512]{1,0:T(8,128)}), f32[1024,512]{1,0:T(8,128)}) %all-gather.3.cloned.1.call-update) | async-done | bytes 2097168 | tf_op jit(solution)/shard_map/all_gather | solution.py:41
  195.8 3.4 reshape.165
  199.2 5.9 %subtract_bitcast_fusion = f32[1,512,2,512]{3,1,2,0:T(8,128)S(1)} fusion(f32[512,2,512]{2,0,1:T(8,128)} %copy.9, f32[512,2,512]{2,1,0:T(2,128)} %reshape.165, f32[512,512]{1,0:T(8,128)S(1)} %convolution_multiply_fusion.1), kind=kOutput, calls=%fused_computation.8 | convolution fusion | flops 3221749760 | bytes 7340032 | tf_op jit(solution)/shard_map/rbc,cjd->rbjd/dot_general | solution.py:82
  205.1 1.2 broadcast_select_fusion.1
  206.3 0.1 bitcast_dynamic-update-slice_fusion
  206.4 2.9 copy.11
  209.3 3.7 squeeze.35
  213.0 3.1 multiply_select_fusion
  216.1 0.0 all-reduce.5.cloned.1.call-start
  216.2 0.5 all-reduce.5.cloned.1.call-update
  216.7 1.1 broadcast_in_dim.61
  217.8 8.2 %all-to-all-start.1 = ((f32[16,32,512]{2,1,0:T(8,128)}), f32[16,32,512]{2,1,0:T(8,128)S(1)}, u32[]{:S(2)}, u32[]{:S(2)}) async-start(f32[16,32,512]{2,1,0:T(8,128)} %broadcast_in_dim.61), calls=%async_computation.2 | async-start | bytes 2097152 | tf_op jit(solution)/shard_map/all_to_all | solution.py:9
  226.0 0.3 all-gather.5.cloned.1.call-start
  226.2 80.7 %reduce-scatter.5.cloned.1.call-done = f32[64,512]{1,0:T(8,128)} async-done(((f32[1024,512]{1,0:T(8,128)}), f32[64,512]{1,0:T(8,128)}) %reduce-scatter.5.cloned.1.call-update) | async-done | bytes 131088 | tf_op jit(solution)/shard_map/reduce_scatter | solution.py:40
  307.6 45.7 %all-reduce.5.cloned.1.call-done = f32[512,512]{1,0:T(8,128)} async-done(((f32[512,512]{1,0:T(8,128)}), f32[512,512]{1,0:T(8,128)}) %all-reduce.5.cloned.1.call-update) | async-done | bytes 1048592 | tf_op jit(solution)/shard_map/psum | solution.py:25
  353.3 3.4 convolution_multiply_fusion
  356.7 23.4 %all-gather.5.cloned.1.call-done = f32[1024,512]{1,0:T(8,128)} async-done(((f32[64,512]{1,0:T(8,128)}), f32[1024,512]{1,0:T(8,128)}) %all-gather.5.cloned.1.call-update) | async-done | bytes 2097168 | tf_op jit(solution)/shard_map/all_gather | solution.py:41
  380.0 3.4 reshape.168
  383.5 6.6 %bitcast_subtract_fusion = f32[1,512,2,512]{3,1,2,0:T(8,128)} fusion(f32[1,512,2,512]{3,1,2,0:T(8,128)S(1)} %bitcast_dynamic-update-slice_fusion, f32[512,2,512]{2,1,0:T(2,128)} %reshape.168, f32[512,512]{1,0:T(8,128)S(1)} %convolution_multiply_fusion), kind=kOutput, calls=%fused_computation.2 | convolution fusion | flops 3221749760 | bytes 7340032 | tf_op jit(solution)/shard_map/rbc,cjd->rbjd/dot_general | solution.py:82
  390.1 2.4 fusion.10
  392.5 1.9 copy.14
  394.4 1.8 copy.15
  (20 shorter events, 0.1 us)
Async XLA Ops:
  7.4 115.8 %reduce-scatter.3.cloned.1.call-start = ((), (), s32[]{:S(2)}) async-start(), calls=%async_computation.5 | async-start | bytes 2228224 | tf_op jit(solution)/shard_map/reduce_scatter | solution.py:40
  12.9 1.6 copy-start
  12.9 149.0 %all-reduce.3.cloned.1.call-start = ((), (), s32[]{:S(2)}) async-start(), calls=%async_computation.4 | async-start | bytes 2097152 | tf_op jit(solution)/shard_map/psum | solution.py:25
  19.8 1.1 copy-start.3
  22.0 140.0 %all-to-all-start = ((f32[16,32,512]{2,1,0:T(8,128)}), f32[16,32,512]{2,1,0:T(8,128)S(1)}, u32[]{:S(2)}, u32[]{:S(2)}) async-start(f32[16,32,512]{2,1,0:T(8,128)} %broadcast_in_dim.55), calls=%async_computation | async-start | bytes 2097152 | tf_op jit(solution)/shard_map/all_to_all | solution.py:9
  37.2 158.6 %all-gather.3.cloned.1.call-start = ((), (), s32[]{:S(2)}) async-start(), calls=%async_computation.6 | async-start | bytes 2228224 | tf_op jit(solution)/shard_map/all_gather | solution.py:41
  123.2 183.7 %reduce-scatter.5.cloned.1.call-start = ((), (), s32[]{:S(2)}) async-start(), calls=%async_computation.8 | async-start | bytes 2228224 | tf_op jit(solution)/shard_map/reduce_scatter | solution.py:40
  123.4 1.8 copy-start.4
  162.0 1.0 copy-start.1
  216.1 137.2 %all-reduce.5.cloned.1.call-start = ((), (), s32[]{:S(2)}) async-start(), calls=%async_computation.7 | async-start | bytes 2097152 | tf_op jit(solution)/shard_map/psum | solution.py:25
  217.8 89.8 %all-to-all-start.1 = ((f32[16,32,512]{2,1,0:T(8,128)}), f32[16,32,512]{2,1,0:T(8,128)S(1)}, u32[]{:S(2)}, u32[]{:S(2)}) async-start(f32[16,32,512]{2,1,0:T(8,128)} %broadcast_in_dim.61), calls=%async_computation.2 | async-start | bytes 2097152 | tf_op jit(solution)/shard_map/all_to_all | solution.py:9
  226.0 154.1 %all-gather.5.cloned.1.call-start = ((), (), s32[]{:S(2)}) async-start(), calls=%async_computation.9 | async-start | bytes 2228224 | tf_op jit(solution)/shard_map/all_gather | solution.py:41
  307.6 45.7 %copy-start.2 = (f32[16,32,512]{2,1,0:T(8,128)}, f32[16,32,512]{2,1,0:T(8,128)S(1)}, u32[]{:S(2)}) copy-start(f32[16,32,512]{2,1,0:T(8,128)S(1)} %all-to-all-done.1) | copy-start | bytes 3145732
Sparse Core Ops, SparseCore 0:
  13.1 110.0 reduce-scatter.2
  125.3 70.4 all-gather.2
  216.2 90.6 reduce-scatter.4
  308.8 71.1 all-gather.4
Sparse Core Ops, SparseCore 1:
  20.9 141.0 all-reduce.2
  219.8 133.4 all-reduce.4
where the time goes:
time: 404 us; the launch traced here: 403 us
  waiting for transfers between devices  298 us (74%)
  local copies, waits for them, and re-layouts  34.7 us (9%)
  starting transfers between devices  24 us (6%)
  matrix products  19.2 us (5%)
  between operations  16 us (4%)
  other arithmetic  11.4 us (3%)
    reduce_scatter x2, waiting for transfers between devices, broadcast_by_parts(): own = lax.psum_scatter(padded, axis, scatter_dimension=0, tiled=True)  167 us
    psum x2, waiting for transfers between devices, spread(): return lax.psum(kept, axis)  78 us
    all_gather x2, waiting for transfers between devices, broadcast_by_parts(): lax.all_gather(own, axis, axis=0, tiled=True)[:len(lines)]  52.8 us
    all_to_all x2, starting transfers between devices, copy_for_each(): return lax.all_to_all(copies, axis, split_axis=0, concat_axis=0, tiled=True)  23.4 us
    dot_general x2, matrix products, outer_update(): jnp.einsum('rbc,cjd->rbjd', lower_part, upper_part, precision=lax.Precisi...  12.4 us
  transfers between devices with their start and end apart: 8, of which 6 were waited for; matrix products, arithmetic and copies ran while one was open for 5% of the time, Pallas kernels for 0%

commit v1 on v0

--- a/solution.py
+++ b/solution.py
@@ -2,6 +2,11 @@
 import jax.numpy as jnp
 from jax import lax
 from jax.sharding import PartitionSpec as P
+
+
+def gather_over(array, mesh_axis, along):
+    repeated = jnp.stack([array] * lax.axis_size(mesh_axis))
+    return jnp.concatenate(lax.all_to_all(repeated, mesh_axis, 0, 0), axis=along)
 
 
 def copy_for_each(value, axis):
@@ -38,7 +43,7 @@
     )
     padded = filled_up(lines, lax.axis_size(axis))
     own = lax.psum_scatter(padded, axis, scatter_dimension=0, tiled=True)
-    return lax.all_gather(own, axis, axis=0, tiled=True)[: len(lines)].reshape(value.shape)
+    return gather_over(own, axis, 0)[: len(lines)].reshape(value.shape)
 
 
 def apply_pivot(column_part, pivot_rows):

time: 404 us -> 582 us (1.44)
  the two profiles are of different devices: /device:TPU:4 before, /device:TPU:1 now
where the time goes in v1:
time: 582 us; the launch traced here: 581 us
  waiting for transfers between devices  342 us (59%)
  blocking collectives  136 us (23%)
  local copies, waits for them, and re-layouts  36.3 us (6%)
  starting transfers between devices  20 us (3%)
  matrix products  18.9 us (3%)
  between operations  16.3 us (3%)
  other arithmetic  11.5 us (2%)
    psum x2, waiting for transfers between devices, spread(): return lax.psum(kept, axis)  284 us
    all_to_all x2, blocking collectives, copy_for_each(): return lax.all_to_all(copies, axis, split_axis=0, concat_axis=0, tiled=True)  136 us
    reduce_scatter x2, waiting for transfers between devices, broadcast_by_parts(): own = lax.psum_scatter(padded, axis, scatter_dimension=0, tiled=True)  57.6 us
    all_to_all x2, starting transfers between devices, gather_over(): lax.all_to_all(repeated, mesh_axis, 0, 0)  19.5 us
    dot_general x2, matrix products, outer_update(): jnp.einsum('rbc,cjd->rbjd', lower_part, upper_part, precision=lax.Precisi...  12.5 us
  transfers between devices with their start and end apart: 6, of which 4 were waited for; matrix products, arithmetic and copies ran while one was open for 3% of the time, Pallas kernels for 0%

profile of v1, /device:TPU:1, one launch (start us, length us, event | category | flops | bytes accessed | tf_op | source)
XLA Modules:
  0.0 581.2 jit_solution(6314038819548555872)
XLA Ops:
  7.4 0.8 slice_bitcast_fusion.4
  8.1 0.6 gather_fusion
  8.8 0.6 gather_fusion.1
  9.5 0.2 mul.56
  9.6 1.7 squeeze_reshape.3
  11.4 1.5 multiply_select_fusion.1
  12.9 0.0 reduce-scatter.3.cloned.1.call-update
  12.9 0.9 copy-done.2
  13.8 0.1 broadcast_in_dim.55
  14.0 70.0 %all_to_all.20 = f32[16,32,512]{2,1,0:T(8,128)} all-to-all(f32[16,32,512]{2,1,0:T(8,128)S(1)} %broadcast_in_dim.55), channel_id=1, replica_groups=mesh['prow'=16,'pcol'=32] {'prow'}, dimensions={0} | all-to-all | bytes 2097152 | tf_op jit(solution)/shard_map/all_to_all | solution.py:14
  84.0 29.2 %reduce-scatter.3.cloned.1.call-done = f32[64,512]{1,0:T(8,128)} async-done(((f32[1024,512]{1,0:T(8,128)}), f32[64,512]{1,0:T(8,128)}) %reduce-scatter.3.cloned.1.call-update) | async-done | bytes 131088 | tf_op jit(solution)/shard_map/reduce_scatter | solution.py:45
  113.2 2.5 stack.4
  115.7 9.4 %all-to-all-start.1 = ((f32[16,64,512]{2,1,0:T(8,128)}), f32[16,64,512]{2,1,0:T(8,128)}, u32[]{:S(2)}, u32[]{:S(2)}) async-start(f32[16,64,512]{2,1,0:T(8,128)} %stack.4), calls=%async_computation.2 | async-start | bytes 4194304 | tf_op jit(solution)/shard_map/all_to_all | solution.py:9
  125.1 0.0 all-reduce.3.cloned.1.call-start
  125.2 2.8 reshape.160
  128.0 2.5 broadcast_select_fusion
  130.5 1.1 copy.28
  131.6 0.0 all-reduce.3.cloned.1.call-update
  131.6 0.2 reduce-scatter.5.cloned.1.call-start
  131.9 0.0 copy-start.3
  131.9 1.8 copy.7
  133.7 0.7 fusion.18
  135.1 3.0 copy.9
  138.1 0.2 mul.63
  138.3 138.1 %all-reduce.3.cloned.1.call-done = f32[512,512]{1,0:T(8,128)} async-done(((f32[512,512]{1,0:T(8,128)}), f32[512,512]{1,0:T(8,128)}) %all-reduce.3.cloned.1.call-update) | async-done | bytes 1048592 | tf_op jit(solution)/shard_map/psum | solution.py:30
  276.4 3.1 convolution_multiply_fusion.1
  279.5 3.4 reshape_reshape.6
  282.9 5.9 %subtract_bitcast_fusion = f32[1,512,2,512]{3,1,2,0:T(8,128)S(1)} fusion(f32[512,2,512]{2,0,1:T(8,128)} %copy.9, f32[512,2,512]{2,1,0:T(2,128)} %reshape_reshape.6, f32[512,512]{1,0:T(8,128)S(1)} %convolution_multiply_fusion.1), kind=kOutput, calls=%fused_computation.8 | convolution fusion | flops 3221749760 | bytes 7340032 | tf_op jit(solution)/shard_map/rbc,cjd->rbjd/dot_general | solution.py:87
  288.8 1.2 broadcast_select_fusion.1
  290.0 0.1 bitcast_dynamic-update-slice_fusion
  290.1 2.9 copy.11
  293.0 3.7 squeeze.35
  296.7 3.1 multiply_select_fusion
  299.8 0.0 reduce-scatter.5.cloned.1.call-update
  299.9 0.1 broadcast_in_dim.61
  300.0 66.4 %all_to_all.21 = f32[16,32,512]{2,1,0:T(8,128)} all-to-all(f32[16,32,512]{2,1,0:T(8,128)S(1)} %broadcast_in_dim.61), channel_id=1, replica_groups=mesh['prow'=16,'pcol'=32] {'prow'}, dimensions={0} | all-to-all | bytes 2097152 | tf_op jit(solution)/shard_map/all_to_all | solution.py:14
  366.4 28.4 %reduce-scatter.5.cloned.1.call-done = f32[64,512]{1,0:T(8,128)} async-done(((f32[1024,512]{1,0:T(8,128)}), f32[64,512]{1,0:T(8,128)}) %reduce-scatter.5.cloned.1.call-update) | async-done | bytes 131088 | tf_op jit(solution)/shard_map/reduce_scatter | solution.py:45
  394.8 2.5 stack.5
  397.3 10.0 %all-to-all-start.3 = ((f32[16,64,512]{2,1,0:T(8,128)}), f32[16,64,512]{2,1,0:T(8,128)}, u32[]{:S(2)}, u32[]{:S(2)}) async-start(f32[16,64,512]{2,1,0:T(8,128)} %stack.5), calls=%async_computation.5 | async-start | bytes 4194304 | tf_op jit(solution)/shard_map/all_to_all | solution.py:9
  407.3 0.3 all-reduce.5.cloned.1.call-start
  407.6 0.3 all-reduce.5.cloned.1.call-update
  408.5 145.6 %all-reduce.5.cloned.1.call-done = f32[512,512]{1,0:T(8,128)} async-done(((f32[512,512]{1,0:T(8,128)}), f32[512,512]{1,0:T(8,128)}) %all-reduce.5.cloned.1.call-update) | async-done | bytes 1048592 | tf_op jit(solution)/shard_map/psum | solution.py:30
  554.2 3.4 convolution_multiply_fusion
  557.6 3.4 reshape_reshape.7
  561.0 6.6 %bitcast_subtract_fusion = f32[1,512,2,512]{3,1,2,0:T(8,128)} fusion(f32[1,512,2,512]{3,1,2,0:T(8,128)S(1)} %bitcast_dynamic-update-slice_fusion, f32[512,2,512]{2,1,0:T(2,128)} %reshape_reshape.7, f32[512,512]{1,0:T(8,128)S(1)} %convolution_multiply_fusion), kind=kOutput, calls=%fused_computation.2 | convolution fusion | flops 3221749760 | bytes 7340032 | tf_op jit(solution)/shard_map/rbc,cjd->rbjd/dot_general | solution.py:87
  567.6 2.4 fusion.10
  570.0 1.9 copy.14
  571.9 1.8 copy.15
  (16 shorter events, 0.1 us)
Async XLA Ops:
  7.4 105.8 %reduce-scatter.3.cloned.1.call-start = ((), (), s32[]{:S(2)}) async-start(), calls=%async_computation.7 | async-start | bytes 2228224 | tf_op jit(solution)/shard_map/reduce_scatter | solution.py:45
  12.9 0.9 copy-start.2
  115.7 9.5 %copy-start = (f32[512,1024]{1,0:T(8,128)S(1)}, f32[512,1024]{1,0:T(8,128)}, u32[]{:S(2)}) copy-start(f32[512,1024]{1,0:T(8,128)} %param.10) | copy-start | bytes 6291460
  115.7 163.8 %all-to-all-start.1 = ((f32[16,64,512]{2,1,0:T(8,128)}), f32[16,64,512]{2,1,0:T(8,128)}, u32[]{:S(2)}, u32[]{:S(2)}) async-start(f32[16,64,512]{2,1,0:T(8,128)} %stack.4), calls=%async_computation.2 | async-start | bytes 4194304 | tf_op jit(solution)/shard_map/all_to_all | solution.py:9
  125.1 151.3 %all-reduce.3.cloned.1.call-start = ((), (), s32[]{:S(2)}) async-start(), calls=%async_computation.6 | async-start | bytes 2097152 | tf_op jit(solution)/shard_map/psum | solution.py:30
  131.6 263.1 %reduce-scatter.5.cloned.1.call-start = ((), (), s32[]{:S(2)}) async-start(), calls=%async_computation.9 | async-start | bytes 2228224 | tf_op jit(solution)/shard_map/reduce_scatter | solution.py:45
  131.9 1.8 copy-start.3
  135.1 141.3 %copy-start.1 = (f32[16,32,512]{2,1,0:T(8,128)S(1)}, f32[16,32,512]{2,1,0:T(8,128)}, u32[]{:S(2)}) copy-start(f32[16,32,512]{2,1,0:T(8,128)} %all_to_all.20) | copy-start | bytes 3145732
  397.3 160.3 %all-to-all-start.3 = ((f32[16,64,512]{2,1,0:T(8,128)}), f32[16,64,512]{2,1,0:T(8,128)}, u32[]{:S(2)}, u32[]{:S(2)}) async-start(f32[16,64,512]{2,1,0:T(8,128)} %stack.5), calls=%async_computation.5 | async-start | bytes 4194304 | tf_op jit(solution)/shard_map/all_to_all | solution.py:9
  407.3 146.9 %all-reduce.5.cloned.1.call-start = ((), (), s32[]{:S(2)}) async-start(), calls=%async_computation.8 | async-start | bytes 2097152 | tf_op jit(solution)/shard_map/psum | solution.py:30
Sparse Core Ops, SparseCore 0:
  13.1 100.1 reduce-scatter.2
  300.0 94.7 reduce-scatter.4
Sparse Core Ops, SparseCore 1:
  131.7 144.6 all-reduce.2
  411.0 143.1 all-reduce.4
